TPU v7x, 32 devices: a whole 2x2x4 slice. The times are simulated.
32 devices in a mesh: study: 2 (over x), ky: 16 (over z, y, core).
Axes of the slice: x: 2, y: 2, z: 4, core: 2. Of those that a mesh axis runs over, the one named last changes fastest.
Arguments:
- kspace: bfloat16 [32, 2, 32, 256, 256], P('study', None, None, 'ky'), parts along dimension 0, may hold values from -6 to 6
- kernel: bfloat16 [2, 768, 64], replicated, may hold values from -0.21875 to 0.21875
- pattern: int32 [32], P('study'), parts along dimension 0, may hold values from 0 to 2
- offsets: int32 [4], replicated, may hold values from -2 to 2
- segment: int32 [256], replicated, may hold values from 0 to 2
- temporal_basis: float32 [5, 16], replicated, may hold values from -1.5 to 1.5
Outputs:
- basis_images: float32 [10, 2, 32, 256, 256], P('study', None, None, 'ky'), parts along dimension 0
There are 2 independent parts, one for each index of `study`. A program takes and returns all parts, laid end to end along the dimension named above; an argument that names none is the same for every part. Nothing has to cross between parts.
All inputs are finite; a program needn't handle non-finite values.
Results may differ from a plain program's by a relative error of at most 0.0003.
Values may be sent and summed in bfloat16 or wider, within the bound.
No kernel may reach another device: no remote copies, remote signals or barrier semaphores. Data moves between devices by JAX's collectives and lax.ppermute only.
A program may use at most 192 MiB of HBM per device.

v0:
```python
import jax
import jax.numpy as jnp
from jax import lax
from jax.sharding import PartitionSpec as P

frame_block = 4


def padded_2(block, sides, width):
    for axis, dim in sides:
        count = lax.axis_size(axis)
        forward = [(i, i + 1) for i in range(count - 1)]
        backward = [(target, source) for source, target in forward]
        low = lax.ppermute(
            lax.slice_in_dim(block, block.shape[dim] - width, None, axis=dim), axis, forward
        )
        high = lax.ppermute(lax.slice_in_dim(block, 0, width, axis=dim), axis, backward)
        block = jnp.concatenate([low, block, high], axis=dim)
    return block


def inverse_rows(spectra):
    row_total = spectra.shape[3]
    row_index = jnp.arange(row_total, dtype=jnp.int32)
    phase_index = row_index[:, None] * row_index[None, :] % row_total
    phase_angle = phase_index.astype(jnp.float32) * (2.0 * jnp.pi / row_total)
    cosine_table = jnp.cos(phase_angle)
    sine_table = jnp.sin(phase_angle)
    real_part = spectra[:, 0]
    imag_part = spectra[:, 1]
    high = lax.Precision.HIGHEST
    out_real = jnp.einsum("yk,mckx->mcxy", cosine_table, real_part, precision=high) - jnp.einsum(
        "yk,mckx->mcxy", sine_table, imag_part, precision=high
    )
    out_imag = jnp.einsum("yk,mckx->mcxy", sine_table, real_part, precision=high) + jnp.einsum(
        "yk,mckx->mcxy", cosine_table, imag_part, precision=high
    )
    scale = 1.0 / jnp.sqrt(jnp.float32(row_total))
    return jnp.stack([out_real, out_imag], axis=1) * scale


def on_device(kspace, kernel, pattern, offsets, segment, temporal_basis):
    frame_total, _, coil_count, row_count, kx_count = kspace.shape
    group_count = kernel.shape[0]
    group_frames = frame_total // group_count
    row_start = lax.axis_index("ky") * row_count
    local_segment = lax.dynamic_slice_in_dim(segment, row_start, row_count)
    acquired = (local_segment[None, :] == pattern[:, None])[:, None, None, :, None]
    zero_fill = jnp.where(acquired, kspace, jnp.zeros_like(kspace))
    padded = padded_2(zero_fill, (("ky", 3),), 1)
    blocks = frame_total // frame_block
    padded_blocks = padded.reshape(blocks, frame_block, 2, coil_count, row_count + 2, kx_count)
    block_group = jnp.arange(blocks, dtype=jnp.int32) * frame_block // group_frames

    def estimate_block(block_item):
        block_data, group_index = block_item
        ky_layers = []
        for ky_tap in range(3):
            ky_slice = block_data[:, :, :, ky_tap : ky_tap + row_count, :]
            ky_layers.append(
                jnp.stack(
                    [
                        jnp.roll(ky_slice, -offsets[kx_tap], axis=4)
                        for kx_tap in range(offsets.shape[0])
                    ],
                    axis=2,
                )
            )
        sources = jnp.stack(ky_layers, axis=2).reshape(frame_block, -1, row_count * kx_count)
        weights = lax.dynamic_index_in_dim(kernel, group_index, 0, keepdims=False)
        return jnp.einsum("io,fir->for", weights, sources, preferred_element_type=jnp.float32)

    estimate = lax.map(estimate_block, (padded_blocks, block_group))
    estimate = estimate.reshape(frame_total, 2, coil_count, row_count, kx_count)
    filled = jnp.where(acquired, kspace.astype(jnp.float32), estimate)
    high = lax.Precision.HIGHEST
    coefficients = jnp.einsum("bf,fpcrx->bpcrx", temporal_basis, filled, precision=high)
    swapped = lax.all_to_all(coefficients, "ky", split_axis=4, concat_axis=3, tiled=True)
    return inverse_rows(swapped)


def solution(mesh):
    return jax.shard_map(
        on_device,
        mesh=mesh,
        in_specs=(P("study", None, None, "ky", None), P(), P("study"), P(), P(), P()),
        out_specs=P("study", None, None, "ky", None),
        check_vma=False,
    )
```

profile of v0, /device:TPU:1, one launch (start us, length us, event | category | flops | bytes accessed | tf_op | source)
XLA Modules:
  0.0 754.4 jit_solution(11994539295915836448)
XLA Ops:
  1.5 7.2 broadcast_select_fusion
  8.7 4.6 fusion.80
  23.3 6.4 collective-permute-done
  31.8 13.5 %pad_maximum_fusion.1 = bf16[16,2,32,18,256]{4,3,2,1,0:T(8,128)(2,1)} fusion(bf16[16,2,32,1,256]{4,3,2,1,0:T(2,128)(2,1)S(1)} %copy.40, bf16[16,2,32,16,256]{4,3,2,1,0:T(8,128)(2,1)} %broadcast_select_fusion, bf16[16,2,32,1,256]{4,3,2,1,0:T(2,128)(2,1)S(1)} %copy.39), kind=kLoop, calls=%fused_computation.61 | loop fusion | flops 28311552 | bytes 18874368 | tf_op jit(solution)/shard_map/concatenate | solution.py:18
  45.4 419.9 %while.12 = (s32[]{:T(128)}, f32[4,4,64,4096]{3,2,1,0:T(8,128)}, bf16[4,4,2,32,18,256]{5,4,3,2,1,0:T(8,128)(2,1)}, s32[]{:T(128)}, s32[]{:T(128)}, /*index=5*/s3...) while((s32[]{:T(128)}, f32[4,4,64,4096]{3,2,1,0:T(8,128)}, ...), condition=%wide.region_1.3_spmd, body=%wide.region_0.2_spmd.sunk | while | flops 1723858944 | bytes 229213552 | solution.py:73
  50.6 7.1 fusion.94
  57.6 9.1 %fusion.95 = (bf16[4,2,1,32,16,256]{5,4,3,2,1,0:T(8,128)(2,1)}, bf16[4,2,1,32,16,256]{5,4,3,2,1,0:T(8,128)(2,1)}, bf16[4,2,1,32,16,256]{5,4,3,2,1,0:T(8,128)(2,1)}, bf16[4,2,1,32,16,256]{5,4,3,2,1,0:T(8,128)(2,1)}) fusion(s32[]{:T(128)S(6)} %select_n.129, bf16[4,2,32,16,256]{4,3,2,1,0:T(8,128)(2,1)S(1)} %get-tuple-element.228, s32[]{:T(128)S(6)} %select_n.131, ...), kind=kLoop, calls=%fused_computation.42.clone.1 | loop fusion | flops 16777216 | bytes 10485776 | tf_op jit(solution)/shard_map/while/body/eval_jaxpr/stack | solution.py:61
  66.7 5.8 maximum_bitcast_fusion.6
  72.6 11.5 %fusion.93 = (bf16[4,2,1,32,16,256]{5,4,3,2,1,0:T(8,128)(2,1)S(1)}, bf16[4,2,1,32,16,256]{5,4,3,2,1,0:T(8,128)(2,1)S(1)}, bf16[4,2,1,32,16,256]{5,4,3,2,1,0:T(8,128)(2,1)S(1)}, bf16[4,2,1,32,16,256]{5,4,3,2,1,0:T(8,128)(2,1)S(1)}) fusion(s32[]{:T(128)S(6)} %select_n.129, bf16[4,2,32,16,256]{4,3,2,1,0:T(8,128)(2,1)} %get-tuple-element.218, ...), kind=kLoop, calls=%fused_computation.34.clone.1 | loop fusion | flops 16777216 | bytes 10485776 | tf_op jit(solution)/shard_map/while/body/eval_jaxpr/stack | solution.py:61
  85.2 10.2 %pad_maximum_fusion.3 = bf16[4,2,3,4,32,16,256]{6,5,4,3,2,1,0:T(8,128)(2,1)} fusion(bf16[4,2,1,4,32,16,256]{6,5,4,3,2,1,0:T(8,128)(2,1)S(1)} %maximum_bitcast_fusion.5, bf16[4,2,1,4,32,16,256]{6,5,4,3,2,1,0:T(8,128)(2,1)S(1)} %get-tuple-element.233, bf16[4,2,1,4,32,16,256]{6,5,4,3,2,1,0:T(8,128)(2,1)S(1)} %get-tuple-element.234), kind=kLoop, calls=%fused_computation.clone.1 | loop fusion | flops 25165824 | bytes 50331648 | tf_op jit(solution)/shard_map/while/body/eval_jaxpr/stack | solution.py:69
  95.4 37.8 %reshape.50 = bf16[4,768,4096]{2,1,0:T(8,128)(2,1)} reshape(bf16[4,2,3,4,32,16,256]{6,5,4,3,2,1,0:T(8,128)(2,1)} %pad_maximum_fusion.3) | data formatting | bytes 50331648 | tf_op jit(solution)/shard_map/while/body/eval_jaxpr/reshape | solution.py:69
  135.8 14.8 %fusion.96 = f32[4,4,64,4096]{3,2,1,0:T(8,128)} fusion(f32[4,4,64,4096]{3,2,1,0:T(8,128)} %get-tuple-element.251, s32[]{:T(128)} %get-tuple-element.250, bf16[4,768,4096]{2,1,0:T(8,128)(2,1)} %reshape.50, bf16[2,768,64]{1,2,0:T(8,128)(2,1)S(1)} %get-tuple-element.273, s32[]{:T(128)S(6)} %select_n.136), kind=kOutput, calls=%fused_computation.29.clone.1 | convolution fusion | flops 1610612736 | bytes 29458948 | tf_op jit(solution)/shard_map/while/body/eval_jaxpr/io,fir->for/dot_general | solution.py:71
  155.5 7.1 fusion.94
  162.5 9.1 %fusion.95 = (bf16[4,2,1,32,16,256]{5,4,3,2,1,0:T(8,128)(2,1)}, bf16[4,2,1,32,16,256]{5,4,3,2,1,0:T(8,128)(2,1)}, bf16[4,2,1,32,16,256]{5,4,3,2,1,0:T(8,128)(2,1)}, bf16[4,2,1,32,16,256]{5,4,3,2,1,0:T(8,128)(2,1)}) fusion(s32[]{:T(128)S(6)} %select_n.129, bf16[4,2,32,16,256]{4,3,2,1,0:T(8,128)(2,1)S(1)} %get-tuple-element.228, s32[]{:T(128)S(6)} %select_n.131, ...), kind=kLoop, calls=%fused_computation.42.clone.1 | loop fusion | flops 16777216 | bytes 10485776 | tf_op jit(solution)/shard_map/while/body/eval_jaxpr/stack | solution.py:61
  171.6 5.8 maximum_bitcast_fusion.6
  177.5 11.5 %fusion.93 = (bf16[4,2,1,32,16,256]{5,4,3,2,1,0:T(8,128)(2,1)S(1)}, bf16[4,2,1,32,16,256]{5,4,3,2,1,0:T(8,128)(2,1)S(1)}, bf16[4,2,1,32,16,256]{5,4,3,2,1,0:T(8,128)(2,1)S(1)}, bf16[4,2,1,32,16,256]{5,4,3,2,1,0:T(8,128)(2,1)S(1)}) fusion(s32[]{:T(128)S(6)} %select_n.129, bf16[4,2,32,16,256]{4,3,2,1,0:T(8,128)(2,1)} %get-tuple-element.218, ...), kind=kLoop, calls=%fused_computation.34.clone.1 | loop fusion | flops 16777216 | bytes 10485776 | tf_op jit(solution)/shard_map/while/body/eval_jaxpr/stack | solution.py:61
  190.1 10.2 %pad_maximum_fusion.3 = bf16[4,2,3,4,32,16,256]{6,5,4,3,2,1,0:T(8,128)(2,1)} fusion(bf16[4,2,1,4,32,16,256]{6,5,4,3,2,1,0:T(8,128)(2,1)S(1)} %maximum_bitcast_fusion.5, bf16[4,2,1,4,32,16,256]{6,5,4,3,2,1,0:T(8,128)(2,1)S(1)} %get-tuple-element.233, bf16[4,2,1,4,32,16,256]{6,5,4,3,2,1,0:T(8,128)(2,1)S(1)} %get-tuple-element.234), kind=kLoop, calls=%fused_computation.clone.1 | loop fusion | flops 25165824 | bytes 50331648 | tf_op jit(solution)/shard_map/while/body/eval_jaxpr/stack | solution.py:69
  200.3 37.8 %reshape.50 = bf16[4,768,4096]{2,1,0:T(8,128)(2,1)} reshape(bf16[4,2,3,4,32,16,256]{6,5,4,3,2,1,0:T(8,128)(2,1)} %pad_maximum_fusion.3) | data formatting | bytes 50331648 | tf_op jit(solution)/shard_map/while/body/eval_jaxpr/reshape | solution.py:69
  240.7 14.7 %fusion.96 = f32[4,4,64,4096]{3,2,1,0:T(8,128)} fusion(f32[4,4,64,4096]{3,2,1,0:T(8,128)} %get-tuple-element.251, s32[]{:T(128)} %get-tuple-element.250, bf16[4,768,4096]{2,1,0:T(8,128)(2,1)} %reshape.50, bf16[2,768,64]{1,2,0:T(8,128)(2,1)S(1)} %get-tuple-element.273, s32[]{:T(128)S(6)} %select_n.136), kind=kOutput, calls=%fused_computation.29.clone.1 | convolution fusion | flops 1610612736 | bytes 29458948 | tf_op jit(solution)/shard_map/while/body/eval_jaxpr/io,fir->for/dot_general | solution.py:71
  260.3 7.1 fusion.94
  267.3 9.1 %fusion.95 = (bf16[4,2,1,32,16,256]{5,4,3,2,1,0:T(8,128)(2,1)}, bf16[4,2,1,32,16,256]{5,4,3,2,1,0:T(8,128)(2,1)}, bf16[4,2,1,32,16,256]{5,4,3,2,1,0:T(8,128)(2,1)}, bf16[4,2,1,32,16,256]{5,4,3,2,1,0:T(8,128)(2,1)}) fusion(s32[]{:T(128)S(6)} %select_n.129, bf16[4,2,32,16,256]{4,3,2,1,0:T(8,128)(2,1)S(1)} %get-tuple-element.228, s32[]{:T(128)S(6)} %select_n.131, ...), kind=kLoop, calls=%fused_computation.42.clone.1 | loop fusion | flops 16777216 | bytes 10485776 | tf_op jit(solution)/shard_map/while/body/eval_jaxpr/stack | solution.py:61
  276.4 5.8 maximum_bitcast_fusion.6
  282.3 11.5 %fusion.93 = (bf16[4,2,1,32,16,256]{5,4,3,2,1,0:T(8,128)(2,1)S(1)}, bf16[4,2,1,32,16,256]{5,4,3,2,1,0:T(8,128)(2,1)S(1)}, bf16[4,2,1,32,16,256]{5,4,3,2,1,0:T(8,128)(2,1)S(1)}, bf16[4,2,1,32,16,256]{5,4,3,2,1,0:T(8,128)(2,1)S(1)}) fusion(s32[]{:T(128)S(6)} %select_n.129, bf16[4,2,32,16,256]{4,3,2,1,0:T(8,128)(2,1)} %get-tuple-element.218, ...), kind=kLoop, calls=%fused_computation.34.clone.1 | loop fusion | flops 16777216 | bytes 10485776 | tf_op jit(solution)/shard_map/while/body/eval_jaxpr/stack | solution.py:61
  294.9 10.2 %pad_maximum_fusion.3 = bf16[4,2,3,4,32,16,256]{6,5,4,3,2,1,0:T(8,128)(2,1)} fusion(bf16[4,2,1,4,32,16,256]{6,5,4,3,2,1,0:T(8,128)(2,1)S(1)} %maximum_bitcast_fusion.5, bf16[4,2,1,4,32,16,256]{6,5,4,3,2,1,0:T(8,128)(2,1)S(1)} %get-tuple-element.233, bf16[4,2,1,4,32,16,256]{6,5,4,3,2,1,0:T(8,128)(2,1)S(1)} %get-tuple-element.234), kind=kLoop, calls=%fused_computation.clone.1 | loop fusion | flops 25165824 | bytes 50331648 | tf_op jit(solution)/shard_map/while/body/eval_jaxpr/stack | solution.py:69
  305.1 37.8 %reshape.50 = bf16[4,768,4096]{2,1,0:T(8,128)(2,1)} reshape(bf16[4,2,3,4,32,16,256]{6,5,4,3,2,1,0:T(8,128)(2,1)} %pad_maximum_fusion.3) | data formatting | bytes 50331648 | tf_op jit(solution)/shard_map/while/body/eval_jaxpr/reshape | solution.py:69
  345.5 14.7 %fusion.96 = f32[4,4,64,4096]{3,2,1,0:T(8,128)} fusion(f32[4,4,64,4096]{3,2,1,0:T(8,128)} %get-tuple-element.251, s32[]{:T(128)} %get-tuple-element.250, bf16[4,768,4096]{2,1,0:T(8,128)(2,1)} %reshape.50, bf16[2,768,64]{1,2,0:T(8,128)(2,1)S(1)} %get-tuple-element.273, s32[]{:T(128)S(6)} %select_n.136), kind=kOutput, calls=%fused_computation.29.clone.1 | convolution fusion | flops 1610612736 | bytes 29458948 | tf_op jit(solution)/shard_map/while/body/eval_jaxpr/io,fir->for/dot_general | solution.py:71
  365.0 7.1 fusion.94
  372.1 9.1 %fusion.95 = (bf16[4,2,1,32,16,256]{5,4,3,2,1,0:T(8,128)(2,1)}, bf16[4,2,1,32,16,256]{5,4,3,2,1,0:T(8,128)(2,1)}, bf16[4,2,1,32,16,256]{5,4,3,2,1,0:T(8,128)(2,1)}, bf16[4,2,1,32,16,256]{5,4,3,2,1,0:T(8,128)(2,1)}) fusion(s32[]{:T(128)S(6)} %select_n.129, bf16[4,2,32,16,256]{4,3,2,1,0:T(8,128)(2,1)S(1)} %get-tuple-element.228, s32[]{:T(128)S(6)} %select_n.131, ...), kind=kLoop, calls=%fused_computation.42.clone.1 | loop fusion | flops 16777216 | bytes 10485776 | tf_op jit(solution)/shard_map/while/body/eval_jaxpr/stack | solution.py:61
  381.2 5.8 maximum_bitcast_fusion.6
  387.1 11.5 %fusion.93 = (bf16[4,2,1,32,16,256]{5,4,3,2,1,0:T(8,128)(2,1)S(1)}, bf16[4,2,1,32,16,256]{5,4,3,2,1,0:T(8,128)(2,1)S(1)}, bf16[4,2,1,32,16,256]{5,4,3,2,1,0:T(8,128)(2,1)S(1)}, bf16[4,2,1,32,16,256]{5,4,3,2,1,0:T(8,128)(2,1)S(1)}) fusion(s32[]{:T(128)S(6)} %select_n.129, bf16[4,2,32,16,256]{4,3,2,1,0:T(8,128)(2,1)} %get-tuple-element.218, ...), kind=kLoop, calls=%fused_computation.34.clone.1 | loop fusion | flops 16777216 | bytes 10485776 | tf_op jit(solution)/shard_map/while/body/eval_jaxpr/stack | solution.py:61
  399.7 10.2 %pad_maximum_fusion.3 = bf16[4,2,3,4,32,16,256]{6,5,4,3,2,1,0:T(8,128)(2,1)} fusion(bf16[4,2,1,4,32,16,256]{6,5,4,3,2,1,0:T(8,128)(2,1)S(1)} %maximum_bitcast_fusion.5, bf16[4,2,1,4,32,16,256]{6,5,4,3,2,1,0:T(8,128)(2,1)S(1)} %get-tuple-element.233, bf16[4,2,1,4,32,16,256]{6,5,4,3,2,1,0:T(8,128)(2,1)S(1)} %get-tuple-element.234), kind=kLoop, calls=%fused_computation.clone.1 | loop fusion | flops 25165824 | bytes 50331648 | tf_op jit(solution)/shard_map/while/body/eval_jaxpr/stack | solution.py:69
  409.9 37.8 %reshape.50 = bf16[4,768,4096]{2,1,0:T(8,128)(2,1)} reshape(bf16[4,2,3,4,32,16,256]{6,5,4,3,2,1,0:T(8,128)(2,1)} %pad_maximum_fusion.3) | data formatting | bytes 50331648 | tf_op jit(solution)/shard_map/while/body/eval_jaxpr/reshape | solution.py:69
  450.2 14.7 %fusion.96 = f32[4,4,64,4096]{3,2,1,0:T(8,128)} fusion(f32[4,4,64,4096]{3,2,1,0:T(8,128)} %get-tuple-element.251, s32[]{:T(128)} %get-tuple-element.250, bf16[4,768,4096]{2,1,0:T(8,128)(2,1)} %reshape.50, bf16[2,768,64]{1,2,0:T(8,128)(2,1)S(1)} %get-tuple-element.273, s32[]{:T(128)S(6)} %select_n.136), kind=kOutput, calls=%fused_computation.29.clone.1 | convolution fusion | flops 1610612736 | bytes 29458948 | tf_op jit(solution)/shard_map/while/body/eval_jaxpr/io,fir->for/dot_general | solution.py:71
  465.3 11.0 %copy.54 = f32[128,8,16,256]{3,2,1,0:T(8,128)S(1)} copy(f32[128,8,16,256]{3,1,2,0:T(8,128)} %bitcast.126) | data formatting | bytes 33554432
  476.3 6.1 convert_select_fusion
  482.5 17.8 %fusion.30 = f32[5,2,32,16,256]{4,0,3,2,1:T(8,128)} fusion(f32[16,2,32,16,256]{4,3,2,1,0:T(8,128)S(1)} %convert_select_fusion, f32[5,16]{1,0:T(8,128)S(1)} %copy-done), kind=kOutput, calls=%fused_computation.64 | convolution fusion | flops 251658240 | bytes 22020416 | tf_op jit(solution)/shard_map/bf,fpcrx->bpcrx/dot_general | solution.py:77
  500.3 14.0 %copy.42 = f32[5,2,32,16,256]{2,3,1,0,4:T(8,128)} copy(f32[5,2,32,16,256]{4,0,3,2,1:T(8,128)} %fusion.30) | data formatting | bytes 10485760 | tf_op jit(solution)/shard_map/bf,fpcrx->bpcrx/dot_general | solution.py:77
  514.2 18.0 %reshape.47 = f32[16,1,81920]{2,1,0:T(1,128)} reshape(f32[256,5,2,16,32]{4,3,2,1,0:T(8,128)} %bitcast.122) | data formatting | bytes 10485760
  532.2 121.4 %all_to_all.18 = f32[16,1,81920]{2,1,0:T(1,128)} all-to-all(f32[16,1,81920]{2,1,0:T(1,128)} %reshape.47), channel_id=1, replica_groups=mesh['study'=2,'ky'=16] {'ky'}, dimensions={0} | all-to-all | bytes 10485760 | tf_op jit(solution)/shard_map/all_to_all | solution.py:78
  654.2 16.9 %reduce = f32[16,81920]{1,0:T(8,128)} reduce(f32[16,1,81920]{2,1,0:T(1,128)} %all_to_all.18, f32[]{:T(128)} %broadcast.61), dimensions={1}, to_apply=%all_to_all.13.reduce_sub_computation | reduce | bytes 10485764 | tf_op jit(solution)/shard_map/all_to_all | solution.py:78
  671.1 18.1 %reshape.48 = f32[256,5,2,16,32]{4,3,2,1,0:T(8,128)} reshape(f32[16,81920]{1,0:T(8,128)} %reduce) | data formatting | bytes 10485760
  689.2 18.5 %copy.44 = f32[5,2,32,16,16,16]{2,5,4,3,1,0:T(8,128)S(1)} copy(f32[5,2,32,16,16,16]{2,4,1,0,5,3:T(8,128)} %bitcast.123) | data formatting | bytes 10485760 | tf_op jit(solution)/shard_map/all_to_all | solution.py:78
  707.7 7.5 fusion.79
  715.3 8.6 %copy.53 = f32[5,1,32,256,16]{3,4,2,0,1:T(8,128)S(1)} copy(f32[5,1,32,256,16]{2,4,3,1,0:T(8,128)} %get-tuple-element.139) | data formatting | bytes 5242880
  723.9 4.8 fusion.35
  728.7 4.7 fusion.33
  733.4 8.7 %copy.52 = f32[5,1,32,256,16]{3,4,2,0,1:T(8,128)S(1)} copy(f32[5,1,32,256,16]{2,4,3,1,0:T(8,128)} %get-tuple-element.138) | data formatting | bytes 5242880
  742.0 5.1 subtract_bitcast_fusion
  (44 shorter events, 45.0 us)
Async XLA Ops:
  0.0 482.5 %copy-start = (f32[5,16]{1,0:T(8,128)S(1)}, f32[5,16]{1,0:T(8,128)}, u32[]{:S(2)}) copy-start(f32[5,16]{1,0:T(8,128)} %param.15) | copy-start | bytes 964
  1.5 7.2 copy-start.3
  8.7 11.3 %copy-start.5 = (s32[4]{0:T(128)S(1)}, s32[4]{0:T(128)}, u32[]{:S(2)}) copy-start(s32[4]{0:T(128)} %param.13) | copy-start | bytes 52
  13.5 16.3 %collective-permute-start = (bf16[16,2,32,1,256]{4,2,3,1,0:T(8,128)(2,1)S(1)}, bf16[16,2,32,1,256]{4,2,3,1,0:T(8,128)(2,1)S(1)}, u32[]{:S(2)}, u32[]{:S(2)}) collective-permute-start(bf16[16,2,32,1,256]{4,2,3,1,0:T(8,128)(2,1)S(1)} %copy.37), channel_id=1, source_target_pairs={{0,1},{1,2},{2,3},{3,4},{4,5},{5,6},{6,7},{7,8},{8,9},{9,10},{10,1... | collective-permute-start | bytes 1572872 | tf_op jit(solution)/shard_map/ppermute | solution.py:14
  18.1 12.6 %collective-permute-start.1 = (bf16[16,2,32,1,256]{4,2,3,1,0:T(8,128)(2,1)S(1)}, bf16[16,2,32,1,256]{4,2,3,1,0:T(8,128)(2,1)S(1)}, u32[]{:S(2)}, u32[]{:S(2)}) collective-permute-start(bf16[16,2,32,1,256]{4,2,3,1,0:T(8,128)(2,1)S(1)} %copy.38), channel_id=1, source_target_pairs={{1,0},{2,1},{3,2},{4,3},{5,4},{6,5},{7,6},{8,7},{9,8},{10,9},{11,1... | collective-permute-start | bytes 1572872 | tf_op jit(solution)/shard_map/ppermute | solution.py:17
  31.8 13.6 %copy-start.2 = (bf16[2,768,64]{1,2,0:T(8,128)(2,1)S(1)}, bf16[2,768,64]{1,2,0:T(8,128)(2,1)}, u32[]{:S(2)}) copy-start(bf16[2,768,64]{1,2,0:T(8,128)(2,1)} %param.11) | copy-start | bytes 589828
  465.3 11.0 %copy-start.4 = (pred[16,16]{1,0:T(8,128)(4,1)S(1)}, pred[16,16]{1,0:T(8,128)(4,1)}, u32[]{:S(2)}) copy-start(pred[16,16]{1,0:T(8,128)(4,1)} %copy-done.3) | copy-start | bytes 772
  742.0 5.1 copy-start.1
where the time goes:
time: 765 us; the launch traced here: 754 us
  local copies, waits for them, and re-layouts  289 us (38%)
  other arithmetic  225 us (29%)
  blocking collectives  121 us (16%)
  matrix products  94.5 us (12%)
  loops' own time  8.59 us (1%)
    reshape x4, local copies, waits for them, and re-layouts, estimate_block(): jnp.stack(ky_layers, axis=2).reshape(frame_block, -1, row_count * kx_count)  151 us
    all_to_all x1, blocking collectives, on_device(): lax.all_to_all(coefficients, 'ky', split_axis=4, concat_axis=3, tiled=True)  121 us
    another operation x12, other arithmetic, estimate_block(): jnp.stack([jnp.roll(ky_slice, -offsets[kx_tap], axis=4) for kx_tap in ran...  111 us
    another operation x12, other arithmetic, estimate_block(): jnp.stack(ky_layers, axis=2).reshape(frame_block, -1, row_count * kx_count)  68.6 us
    unnamed x17, local copies, waits for them, and re-layouts  64.4 us
    dot_general x4, matrix products, estimate_block(): jnp.einsum('io,fir->for', weights, sources, preferred_element_type=jnp.fl...  58.8 us
    all_to_all x2, local copies, waits for them, and re-layouts, on_device(): lax.all_to_all(coefficients, 'ky', split_axis=4, concat_axis=3, tiled=True)  19 us
    dot_general x1, matrix products, on_device(): jnp.einsum('bf,fpcrx->bpcrx', temporal_basis, filled, precision=high)  17.8 us
  transfers between devices with their start and end apart: 2, of which 1 were waited for; matrix products, arithmetic and copies ran while one was open for 0% of the time, Pallas kernels for 0%

commit v1 on v0

--- a/solution.py
+++ b/solution.py
@@ -4,6 +4,29 @@
 from jax.sharding import PartitionSpec as P
 
 frame_block = 4
+
+
+def split_up(x, dim, size):
+    before, after = (x.shape[:dim], x.shape[dim + 1 :])
+    return jnp.moveaxis(x.reshape(*before, size, -1, *after), dim, 0)
+
+
+def joined_along(blocks, dim):
+    blocks = jnp.moveaxis(blocks, 0, dim)
+    shape = blocks.shape
+    return blocks.reshape(*shape[:dim], shape[dim] * shape[dim + 1], *shape[dim + 2 :])
+
+
+def exchange_directly(x, axis, split_dim, concat_dim):
+    size, index = (lax.axis_size(axis), lax.axis_index(axis))
+    blocks = split_up(x, split_dim, size)
+    out = blocks
+    for turn in range(1, size):
+        target, source = ((index + turn) % size, (index - turn) % size)
+        sent = lax.dynamic_index_in_dim(blocks, target, 0)
+        theirs = lax.ppermute(sent, axis, [(i, (i + turn) % size) for i in range(size)])
+        out = lax.dynamic_update_slice_in_dim(out, theirs, source, axis=0)
+    return joined_along(out, concat_dim)
 
 
 def padded_2(block, sides, width):
@@ -75,7 +98,7 @@
     filled = jnp.where(acquired, kspace.astype(jnp.float32), estimate)
     high = lax.Precision.HIGHEST
     coefficients = jnp.einsum("bf,fpcrx->bpcrx", temporal_basis, filled, precision=high)
-    swapped = lax.all_to_all(coefficients, "ky", split_axis=4, concat_axis=3, tiled=True)
+    swapped = exchange_directly(coefficients, "ky", 4, 3)
     return inverse_rows(swapped)
 
 

time: 765 us -> 1090 us (1.42)
  the two profiles are of different devices: /device:TPU:1 before, /device:TPU:9 now
where the time goes in v1:
time: 1090 us; the launch traced here: 1080 us
  starting transfers between devices  354 us (32%)
  local copies, waits for them, and re-layouts  284 us (26%)
  other arithmetic  208 us (19%)
  waiting for transfers between devices  128 us (12%)
  matrix products  94.6 us (9%)
    ppermute x15, starting transfers between devices, exchange_directly(): lax.ppermute(sent, axis, [(i, (i + turn) % size) for i in range(size)])  348 us
    reshape x4, local copies, waits for them, and re-layouts, estimate_block(): jnp.stack(ky_layers, axis=2).reshape(frame_block, -1, row_count * kx_count)  151 us
    ppermute x15, waiting for transfers between devices, exchange_directly(): lax.ppermute(sent, axis, [(i, (i + turn) % size) for i in range(size)])  121 us
    another operation x12, other arithmetic, estimate_block(): jnp.stack([jnp.roll(ky_slice, -offsets[kx_tap], axis=4) for kx_tap in ran...  111 us
    another operation x12, other arithmetic, estimate_block(): jnp.stack(ky_layers, axis=2).reshape(frame_block, -1, row_count * kx_count)  69.1 us
    dot_general x4, matrix products, estimate_block(): jnp.einsum('io,fir->for', weights, sources, preferred_element_type=jnp.fl...  58.9 us
    unnamed x27, local copies, waits for them, and re-layouts  28.1 us
    dynamic_update_slice x15, local copies, waits for them, and re-layouts, exchange_directly(): out = lax.dynamic_update_slice_in_dim(out, theirs, source, axis=0)  22.3 us
  transfers between devices with their start and end apart: 17, of which 6 were waited for; matrix products, arithmetic and copies ran while one was open for 2% of the time, Pallas kernels for 0%

profile of v1, /device:TPU:9, one launch (start us, length us, event | category | flops | bytes accessed | tf_op | source)
XLA Modules:
  0.0 1080.1 jit_solution(7008556805317428895)
XLA Ops:
  1.5 7.3 broadcast_select_fusion
  22.7 7.0 collective-permute-done.1
  31.8 13.5 %pad_maximum_fusion.1 = bf16[16,2,32,18,256]{4,3,2,1,0:T(8,128)(2,1)} fusion(bf16[16,2,32,1,256]{4,3,2,1,0:T(2,128)(2,1)S(1)} %copy.28, bf16[16,2,32,16,256]{4,3,2,1,0:T(8,128)(2,1)} %broadcast_select_fusion, bf16[16,2,32,1,256]{4,3,2,1,0:T(2,128)(2,1)S(1)} %copy.27), kind=kLoop, calls=%fused_computation.61 | loop fusion | flops 28311552 | bytes 18874368 | tf_op jit(solution)/shard_map/concatenate | solution.py:41
  45.3 425.0 %while.12 = (s32[]{:T(128)}, f32[4,4,64,4096]{3,2,1,0:T(8,128)}, bf16[4,4,2,32,18,256]{5,4,3,2,1,0:T(8,128)(2,1)}, s32[]{:T(128)}, s32[]{:T(128)}, /*index=5*/s3...) while((s32[]{:T(128)}, f32[4,4,64,4096]{3,2,1,0:T(8,128)}, ...), condition=%wide.region_1.3_spmd, body=%wide.region_0.2_spmd.sunk | while | flops 1723858944 | bytes 237601680 | solution.py:96
  51.1 11.5 %fusion.93 = (bf16[4,2,1,32,16,256]{5,4,3,2,1,0:T(8,128)(2,1)S(1)}, bf16[4,2,1,32,16,256]{5,4,3,2,1,0:T(8,128)(2,1)S(1)}, bf16[4,2,1,32,16,256]{5,4,3,2,1,0:T(8,128)(2,1)S(1)}, bf16[4,2,1,32,16,256]{5,4,3,2,1,0:T(8,128)(2,1)S(1)}) fusion(s32[]{:T(128)S(6)} %select_n.402, bf16[4,2,32,16,256]{4,3,2,1,0:T(8,128)(2,1)} %get-tuple-element.233, ...), kind=kLoop, calls=%fused_computation.34.clone.1 | loop fusion | flops 16777216 | bytes 10485776 | tf_op jit(solution)/shard_map/while/body/eval_jaxpr/stack | solution.py:84
  64.2 7.1 fusion.94
  71.3 9.1 fusion.95
  80.4 5.8 maximum_bitcast_fusion.6
  86.2 10.3 pad_maximum_fusion.3
  96.6 37.8 %reshape.71 = bf16[4,768,4096]{2,1,0:T(8,128)(2,1)} reshape(bf16[4,2,3,4,32,16,256]{6,5,4,3,2,1,0:T(8,128)(2,1)} %pad_maximum_fusion.3) | data formatting | bytes 50331648 | tf_op jit(solution)/shard_map/while/body/eval_jaxpr/reshape | solution.py:92
  136.9 14.8 %fusion.96 = f32[4,4,64,4096]{3,2,1,0:T(8,128)} fusion(f32[4,4,64,4096]{3,2,1,0:T(8,128)} %get-tuple-element.266, s32[]{:T(128)S(6)} %copy.48, bf16[4,768,4096]{2,1,0:T(8,128)(2,1)} %reshape.71, bf16[2,768,64]{1,2,0:T(8,128)(2,1)S(1)} %get-tuple-element.288, s32[]{:T(128)S(6)} %select_n.409), kind=kOutput, calls=%fused_computation.29.clone.1 | convolution fusion | flops 1610612736 | bytes 29458440 | tf_op jit(solution)/shard_map/while/body/eval_jaxpr/io,fir->for/dot_general | solution.py:94
  157.2 11.5 %fusion.93 = (bf16[4,2,1,32,16,256]{5,4,3,2,1,0:T(8,128)(2,1)S(1)}, bf16[4,2,1,32,16,256]{5,4,3,2,1,0:T(8,128)(2,1)S(1)}, bf16[4,2,1,32,16,256]{5,4,3,2,1,0:T(8,128)(2,1)S(1)}, bf16[4,2,1,32,16,256]{5,4,3,2,1,0:T(8,128)(2,1)S(1)}) fusion(s32[]{:T(128)S(6)} %select_n.402, bf16[4,2,32,16,256]{4,3,2,1,0:T(8,128)(2,1)} %get-tuple-element.233, ...), kind=kLoop, calls=%fused_computation.34.clone.1 | loop fusion | flops 16777216 | bytes 10485776 | tf_op jit(solution)/shard_map/while/body/eval_jaxpr/stack | solution.py:84
  170.3 7.1 fusion.94
  177.4 9.1 fusion.95
  192.4 10.3 pad_maximum_fusion.3
  202.7 37.8 %reshape.71 = bf16[4,768,4096]{2,1,0:T(8,128)(2,1)} reshape(bf16[4,2,3,4,32,16,256]{6,5,4,3,2,1,0:T(8,128)(2,1)} %pad_maximum_fusion.3) | data formatting | bytes 50331648 | tf_op jit(solution)/shard_map/while/body/eval_jaxpr/reshape | solution.py:92
  243.0 14.7 %fusion.96 = f32[4,4,64,4096]{3,2,1,0:T(8,128)} fusion(f32[4,4,64,4096]{3,2,1,0:T(8,128)} %get-tuple-element.266, s32[]{:T(128)S(6)} %copy.48, bf16[4,768,4096]{2,1,0:T(8,128)(2,1)} %reshape.71, bf16[2,768,64]{1,2,0:T(8,128)(2,1)S(1)} %get-tuple-element.288, s32[]{:T(128)S(6)} %select_n.409), kind=kOutput, calls=%fused_computation.29.clone.1 | convolution fusion | flops 1610612736 | bytes 29458440 | tf_op jit(solution)/shard_map/while/body/eval_jaxpr/io,fir->for/dot_general | solution.py:94
  263.3 11.5 %fusion.93 = (bf16[4,2,1,32,16,256]{5,4,3,2,1,0:T(8,128)(2,1)S(1)}, bf16[4,2,1,32,16,256]{5,4,3,2,1,0:T(8,128)(2,1)S(1)}, bf16[4,2,1,32,16,256]{5,4,3,2,1,0:T(8,128)(2,1)S(1)}, bf16[4,2,1,32,16,256]{5,4,3,2,1,0:T(8,128)(2,1)S(1)}) fusion(s32[]{:T(128)S(6)} %select_n.402, bf16[4,2,32,16,256]{4,3,2,1,0:T(8,128)(2,1)} %get-tuple-element.233, ...), kind=kLoop, calls=%fused_computation.34.clone.1 | loop fusion | flops 16777216 | bytes 10485776 | tf_op jit(solution)/shard_map/while/body/eval_jaxpr/stack | solution.py:84
  276.4 7.1 fusion.94
  283.5 9.1 fusion.95
  298.5 10.3 pad_maximum_fusion.3
  308.8 37.8 %reshape.71 = bf16[4,768,4096]{2,1,0:T(8,128)(2,1)} reshape(bf16[4,2,3,4,32,16,256]{6,5,4,3,2,1,0:T(8,128)(2,1)} %pad_maximum_fusion.3) | data formatting | bytes 50331648 | tf_op jit(solution)/shard_map/while/body/eval_jaxpr/reshape | solution.py:92
  349.1 14.7 %fusion.96 = f32[4,4,64,4096]{3,2,1,0:T(8,128)} fusion(f32[4,4,64,4096]{3,2,1,0:T(8,128)} %get-tuple-element.266, s32[]{:T(128)S(6)} %copy.48, bf16[4,768,4096]{2,1,0:T(8,128)(2,1)} %reshape.71, bf16[2,768,64]{1,2,0:T(8,128)(2,1)S(1)} %get-tuple-element.288, s32[]{:T(128)S(6)} %select_n.409), kind=kOutput, calls=%fused_computation.29.clone.1 | convolution fusion | flops 1610612736 | bytes 29458440 | tf_op jit(solution)/shard_map/while/body/eval_jaxpr/io,fir->for/dot_general | solution.py:94
  369.4 11.5 %fusion.93 = (bf16[4,2,1,32,16,256]{5,4,3,2,1,0:T(8,128)(2,1)S(1)}, bf16[4,2,1,32,16,256]{5,4,3,2,1,0:T(8,128)(2,1)S(1)}, bf16[4,2,1,32,16,256]{5,4,3,2,1,0:T(8,128)(2,1)S(1)}, bf16[4,2,1,32,16,256]{5,4,3,2,1,0:T(8,128)(2,1)S(1)}) fusion(s32[]{:T(128)S(6)} %select_n.402, bf16[4,2,32,16,256]{4,3,2,1,0:T(8,128)(2,1)} %get-tuple-element.233, ...), kind=kLoop, calls=%fused_computation.34.clone.1 | loop fusion | flops 16777216 | bytes 10485776 | tf_op jit(solution)/shard_map/while/body/eval_jaxpr/stack | solution.py:84
  382.5 7.1 fusion.94
  389.6 9.1 fusion.95
  404.5 10.3 pad_maximum_fusion.3
  414.9 37.8 %reshape.71 = bf16[4,768,4096]{2,1,0:T(8,128)(2,1)} reshape(bf16[4,2,3,4,32,16,256]{6,5,4,3,2,1,0:T(8,128)(2,1)} %pad_maximum_fusion.3) | data formatting | bytes 50331648 | tf_op jit(solution)/shard_map/while/body/eval_jaxpr/reshape | solution.py:92
  455.2 14.7 %fusion.96 = f32[4,4,64,4096]{3,2,1,0:T(8,128)} fusion(f32[4,4,64,4096]{3,2,1,0:T(8,128)} %get-tuple-element.266, s32[]{:T(128)S(6)} %copy.48, bf16[4,768,4096]{2,1,0:T(8,128)(2,1)} %reshape.71, bf16[2,768,64]{1,2,0:T(8,128)(2,1)S(1)} %get-tuple-element.288, s32[]{:T(128)S(6)} %select_n.409), kind=kOutput, calls=%fused_computation.29.clone.1 | convolution fusion | flops 1610612736 | bytes 29458440 | tf_op jit(solution)/shard_map/while/body/eval_jaxpr/io,fir->for/dot_general | solution.py:94
  470.3 11.0 %copy.40 = f32[128,8,16,256]{3,2,1,0:T(8,128)S(1)} copy(f32[128,8,16,256]{3,1,2,0:T(8,128)} %bitcast.156) | data formatting | bytes 33554432
  481.3 6.1 convert_select_fusion
  487.5 17.8 %fusion.30 = f32[5,2,32,16,256]{4,0,3,2,1:T(8,128)} fusion(f32[16,2,32,16,256]{4,3,2,1,0:T(8,128)S(1)} %convert_select_fusion, f32[5,16]{1,0:T(8,128)S(1)} %copy-done), kind=kOutput, calls=%fused_computation.64 | convolution fusion | flops 251658240 | bytes 22020416 | tf_op jit(solution)/shard_map/bf,fpcrx->bpcrx/dot_general | solution.py:100
  505.3 15.1 %copy.30 = f32[5,2,32,16,256]{2,4,3,1,0:T(8,128)} copy(f32[5,2,32,16,256]{4,0,3,2,1:T(8,128)} %fusion.30) | data formatting | bytes 10485760 | tf_op jit(solution)/shard_map/bf,fpcrx->bpcrx/dot_general | solution.py:100
  520.4 13.4 %dynamic-slice_bitcast_fusion.1 = (f32[1,5,2,32,16,16]{3,5,0,4,2,1:T(8,128)S(1)}, f32[1,5,2,32,16,16]{3,5,0,4,2,1:T(8,128)S(1)}, f32[1,5,2,32,16,16]{3,5,0,4,2,1...) fusion(f32[5,2,32,16,16,16]{2,5,4,3,1,0:T(8,128)} %bitcast.150,, ...), kind=kLoop, calls=%fused_computation.75 | loop fusion | bytes 9830460 | tf_op jit(solution)/shard_map/jit(dynamic_index_in_dim)/dynamic_slice | solution.py:26
  539.4 24.3 %collective-permute-done.2 = f32[1,5,2,32,16,16]{3,5,0,4,2,1:T(8,128)} collective-permute-done((f32[1,5,2,32,16,16]{3,5,0,4,2,1:T(8,128)}, f32[1,5,2,32,16,16]{3,5,0,4,2,1:T(8,128)}, u32[]{:S(2)}, u32[]{:S(2)}) %collective-permute-start.2) | collective-permute-done | bytes 327712 | tf_op jit(solution)/shard_map/ppermute | solution.py:27
  566.2 25.9 %collective-permute-done.3 = f32[1,5,2,32,16,16]{3,5,0,4,2,1:T(8,128)} collective-permute-done((f32[1,5,2,32,16,16]{3,5,0,4,2,1:T(8,128)}, f32[1,5,2,32,16,16]{3,5,0,4,2,1:T(8,128)}, u32[]{:S(2)}, u32[]{:S(2)}) %collective-permute-start.3) | collective-permute-done | bytes 327712 | tf_op jit(solution)/shard_map/ppermute | solution.py:27
  599.4 26.1 %collective-permute-start.10 = (f32[1,5,2,32,16,16]{3,5,0,4,2,1:T(8,128)S(1)}, f32[1,5,2,32,16,16]{3,5,0,4,2,1:T(8,128)S(1)}, u32[]{:S(2)}, u32[]{:S(2)}) collective-permute-start(f32[1,5,2,32,16,16]{3,5,0,4,2,1:T(8,128)S(1)} %copy-done.7), channel_id=1, source_target_pairs={{0,9},{1,10},{2,11},{3,12},{4,13},{5,14},{6,15},{7,0},{8,1},{9,2},... | collective-permute-start | bytes 983048 | tf_op jit(solution)/shard_map/ppermute | solution.py:27
  626.7 34.3 %collective-permute-start.11 = (f32[1,5,2,32,16,16]{3,5,0,4,2,1:T(8,128)S(1)}, f32[1,5,2,32,16,16]{3,5,0,4,2,1:T(8,128)S(1)}, u32[]{:S(2)}, u32[]{:S(2)}) collective-permute-start(f32[1,5,2,32,16,16]{3,5,0,4,2,1:T(8,128)S(1)} %copy-done.6), channel_id=1, source_target_pairs={{0,10},{1,11},{2,12},{3,13},{4,14},{5,15},{6,0},{7,1},{8,2},{9,3},... | collective-permute-start | bytes 983048 | tf_op jit(solution)/shard_map/ppermute | solution.py:27
  662.2 27.2 %collective-permute-done.7 = f32[1,5,2,32,16,16]{3,5,0,4,2,1:T(8,128)S(1)} collective-permute-done((f32[1,5,2,32,16,16]{3,5,0,4,2,1:T(8,128)}, f32[1,5,2,32,16,16]{3,5,0,4,2,1:T(8,128)S(1)}, u32[]{:S(2)}, u32[]{:S(2)}) %collective-permute-start.7) | collective-permute-done | bytes 327712 | tf_op jit(solution)/shard_map/ppermute | solution.py:27
  689.5 95.7 %collective-permute-start.12 = (f32[1,5,2,32,16,16]{3,5,0,4,2,1:T(8,128)S(1)}, f32[1,5,2,32,16,16]{3,5,0,4,2,1:T(8,128)S(1)}, u32[]{:S(2)}, u32[]{:S(2)}) collective-permute-start(f32[1,5,2,32,16,16]{3,5,0,4,2,1:T(8,128)S(1)} %copy-done.5), channel_id=1, source_target_pairs={{0,11},{1,12},{2,13},{3,14},{4,15},{5,0},{6,1},{7,2},{8,3},{9,4},{... | collective-permute-start | bytes 983048 | tf_op jit(solution)/shard_map/ppermute | solution.py:27
  786.4 80.1 %collective-permute-start.13 = (f32[1,5,2,32,16,16]{3,5,0,4,2,1:T(8,128)S(1)}, f32[1,5,2,32,16,16]{3,5,0,4,2,1:T(8,128)S(1)}, u32[]{:S(2)}, u32[]{:S(2)}) collective-permute-start(f32[1,5,2,32,16,16]{3,5,0,4,2,1:T(8,128)S(1)} %copy-done.4), channel_id=1, source_target_pairs={{0,12},{1,13},{2,14},{3,15},{4,0},{5,1},{6,2},{7,3},{8,4},{9,5},{1... | collective-permute-start | bytes 983048 | tf_op jit(solution)/shard_map/ppermute | solution.py:27
  867.7 62.7 %collective-permute-start.14 = (f32[1,5,2,32,16,16]{3,5,0,4,2,1:T(8,128)S(1)}, f32[1,5,2,32,16,16]{3,5,0,4,2,1:T(8,128)S(1)}, u32[]{:S(2)}, u32[]{:S(2)}) collective-permute-start(f32[1,5,2,32,16,16]{3,5,0,4,2,1:T(8,128)S(1)} %copy-done.3), channel_id=1, source_target_pairs={{0,13},{1,14},{2,15},{3,0},{4,1},{5,2},{6,3},{7,4},{8,5},{9,6},{10... | collective-permute-start | bytes 983048 | tf_op jit(solution)/shard_map/ppermute | solution.py:27
  933.0 41.0 %collective-permute-start.16 = (f32[1,5,2,32,16,16]{3,5,0,4,2,1:T(8,128)S(1)}, f32[1,5,2,32,16,16]{3,5,0,4,2,1:T(8,128)S(1)}, u32[]{:S(2)}, u32[]{:S(2)}) collective-permute-start(f32[1,5,2,32,16,16]{3,5,0,4,2,1:T(8,128)S(1)} %get-tuple-element.140), channel_id=1, source_target_pairs={{0,15},{1,0},{2,1},{3,2},{4,3},{5,4},{6,5},{7,6},{8,7},{9,8},{10,9... | collective-permute-start | bytes 983048 | tf_op jit(solution)/shard_map/ppermute | solution.py:27
  979.0 41.1 %collective-permute-done.15 = f32[1,5,2,32,16,16]{3,5,0,4,2,1:T(8,128)S(1)} collective-permute-done((f32[1,5,2,32,16,16]{3,5,0,4,2,1:T(8,128)S(1)}, f32[1,5,2,32,16,16]{3,5,0,4,2,1:T(8,128)S(1)}, u32[]{:S(2)}, u32[]{:S(2)}) %collective-permute-start.15) | collective-permute-done | bytes 327712 | tf_op jit(solution)/shard_map/ppermute | solution.py:27
  1025.2 8.4 copy.31
  1033.6 7.6 fusion.79
  1041.2 8.4 copy.39
  1059.1 8.6 copy.38
  (105 shorter events, 117.5 us)
Async XLA Ops:
  0.0 487.5 %copy-start = (f32[5,16]{1,0:T(8,128)S(1)}, f32[5,16]{1,0:T(8,128)}, u32[]{:S(2)}) copy-start(f32[5,16]{1,0:T(8,128)} %param.15) | copy-start | bytes 964
  1.5 7.3 copy-start.10
  8.8 10.7 copy-start.12
  13.5 16.2 %collective-permute-start.1 = (bf16[16,2,32,1,256]{4,2,3,1,0:T(8,128)(2,1)S(1)}, bf16[16,2,32,1,256]{4,2,3,1,0:T(8,128)(2,1)S(1)}, u32[]{:S(2)}, u32[]{:S(2)}) collective-permute-start(bf16[16,2,32,1,256]{4,2,3,1,0:T(8,128)(2,1)S(1)} %copy.26), channel_id=1, source_target_pairs={{1,0},{2,1},{3,2},{4,3},{5,4},{6,5},{7,6},{8,7},{9,8},{10,9},{11,1... | collective-permute-start | bytes 1572872 | tf_op jit(solution)/shard_map/ppermute | solution.py:40
  16.2 14.5 %collective-permute-start = (bf16[16,2,32,1,256]{4,2,3,1,0:T(8,128)(2,1)S(1)}, bf16[16,2,32,1,256]{4,2,3,1,0:T(8,128)(2,1)S(1)}, u32[]{:S(2)}, u32[]{:S(2)}) collective-permute-start(bf16[16,2,32,1,256]{4,2,3,1,0:T(8,128)(2,1)S(1)} %copy.25), channel_id=1, source_target_pairs={{0,1},{1,2},{2,3},{3,4},{4,5},{5,6},{6,7},{7,8},{8,9},{9,10},{10,1... | collective-permute-start | bytes 1572872 | tf_op jit(solution)/shard_map/ppermute | solution.py:37
  31.8 13.5 %copy-start.9 = (bf16[2,768,64]{1,2,0:T(8,128)(2,1)S(1)}, bf16[2,768,64]{1,2,0:T(8,128)(2,1)}, u32[]{:S(2)}) copy-start(bf16[2,768,64]{1,2,0:T(8,128)(2,1)} %param.11) | copy-start | bytes 589828
  62.6 1.6 copy-start.1
  168.8 1.6 copy-start.1
  274.9 1.6 copy-start.1
  380.9 1.6 copy-start.1
  470.3 11.0 %copy-start.11 = (pred[16,16]{1,0:T(8,128)(4,1)S(1)}, pred[16,16]{1,0:T(8,128)(4,1)}, u32[]{:S(2)}) copy-start(pred[16,16]{1,0:T(8,128)(4,1)} %copy-done.10) | copy-start | bytes 772
  533.8 29.9 %collective-permute-start.2 = (f32[1,5,2,32,16,16]{3,5,0,4,2,1:T(8,128)}, f32[1,5,2,32,16,16]{3,5,0,4,2,1:T(8,128)}, u32[]{:S(2)}, u32[]{:S(2)}) collective-permute-start(f32[1,5,2,32,16,16]{3,5,0,4,2,1:T(8,128)} %get-tuple-element.154), channel_id=1, source_target_pairs={{0,1},{1,2},{2,3},{3,4},{4,5},{5,6},{6,7},{7,8},{8,9},{9,10},{10,1... | collective-permute-start | bytes 983048 | tf_op jit(solution)/shard_map/ppermute | solution.py:27
  535.4 56.7 %collective-permute-start.3 = (f32[1,5,2,32,16,16]{3,5,0,4,2,1:T(8,128)}, f32[1,5,2,32,16,16]{3,5,0,4,2,1:T(8,128)}, u32[]{:S(2)}, u32[]{:S(2)}) collective-permute-start(f32[1,5,2,32,16,16]{3,5,0,4,2,1:T(8,128)} %get-tuple-element.153), channel_id=1, source_target_pairs={{0,2},{1,3},{2,4},{3,5},{4,6},{5,7},{6,8},{7,9},{8,10},{9,11},{10,... | collective-permute-start | bytes 983048 | tf_op jit(solution)/shard_map/ppermute | solution.py:27
  535.4 59.2 %collective-permute-start.4 = (f32[1,5,2,32,16,16]{3,5,0,4,2,1:T(8,128)}, f32[1,5,2,32,16,16]{3,5,0,4,2,1:T(8,128)}, u32[]{:S(2)}, u32[]{:S(2)}) collective-permute-start(f32[1,5,2,32,16,16]{3,5,0,4,2,1:T(8,128)} %get-tuple-element.152), channel_id=1, source_target_pairs={{0,3},{1,4},{2,5},{3,6},{4,7},{5,8},{6,9},{7,10},{8,11},{9,12},{10... | collective-permute-start | bytes 983048 | tf_op jit(solution)/shard_map/ppermute | solution.py:27
  537.0 57.6 %copy-start.8 = (f32[1,5,2,32,16,16]{3,5,0,4,2,1:T(8,128)S(1)}, f32[1,5,2,32,16,16]{3,5,0,4,2,1:T(8,128)}, u32[]{:S(2)}) copy-start(f32[1,5,2,32,16,16]{3,5,0,4,2,1:T(8,128)} %get-tuple-element.147) | copy-start | bytes 983044
  537.0 62.3 %copy-start.7 = (f32[1,5,2,32,16,16]{3,5,0,4,2,1:T(8,128)S(1)}, f32[1,5,2,32,16,16]{3,5,0,4,2,1:T(8,128)}, u32[]{:S(2)}) copy-start(f32[1,5,2,32,16,16]{3,5,0,4,2,1:T(8,128)} %get-tuple-element.146) | copy-start | bytes 983044
  537.0 62.3 %collective-permute-start.5 = (f32[1,5,2,32,16,16]{3,5,0,4,2,1:T(8,128)}, f32[1,5,2,32,16,16]{3,5,0,4,2,1:T(8,128)S(1)}, u32[]{:S(2)}, u32[]{:S(2)}) collective-permute-start(f32[1,5,2,32,16,16]{3,5,0,4,2,1:T(8,128)} %get-tuple-element.151), channel_id=1, source_target_pairs={{0,4},{1,5},{2,6},{3,7},{4,8},{5,9},{6,10},{7,11},{8,12},{9,13},{1... | collective-permute-start | bytes 983048 | tf_op jit(solution)/shard_map/ppermute | solution.py:27
  537.1 89.6 %collective-permute-start.6 = (f32[1,5,2,32,16,16]{3,5,0,4,2,1:T(8,128)}, f32[1,5,2,32,16,16]{3,5,0,4,2,1:T(8,128)S(1)}, u32[]{:S(2)}, u32[]{:S(2)}) collective-permute-start(f32[1,5,2,32,16,16]{3,5,0,4,2,1:T(8,128)} %get-tuple-element.150), channel_id=1, source_target_pairs={{0,5},{1,6},{2,7},{3,8},{4,9},{5,10},{6,11},{7,12},{8,13},{9,14},{... | collective-permute-start | bytes 983048 | tf_op jit(solution)/shard_map/ppermute | solution.py:27
  563.7 125.8 %collective-permute-start.7 = (f32[1,5,2,32,16,16]{3,5,0,4,2,1:T(8,128)}, f32[1,5,2,32,16,16]{3,5,0,4,2,1:T(8,128)S(1)}, u32[]{:S(2)}, u32[]{:S(2)}) collective-permute-start(f32[1,5,2,32,16,16]{3,5,0,4,2,1:T(8,128)} %get-tuple-element.149), channel_id=1, source_target_pairs={{0,6},{1,7},{2,8},{3,9},{4,10},{5,11},{6,12},{7,13},{8,14},{9,15},... | collective-permute-start | bytes 983048 | tf_op jit(solution)/shard_map/ppermute | solution.py:27
  566.2 60.5 %copy-start.6 = (f32[1,5,2,32,16,16]{3,5,0,4,2,1:T(8,128)S(1)}, f32[1,5,2,32,16,16]{3,5,0,4,2,1:T(8,128)}, u32[]{:S(2)}) copy-start(f32[1,5,2,32,16,16]{3,5,0,4,2,1:T(8,128)} %get-tuple-element.145) | copy-start | bytes 983044
  592.1 194.4 %collective-permute-start.8 = (f32[1,5,2,32,16,16]{3,5,0,4,2,1:T(8,128)}, f32[1,5,2,32,16,16]{3,5,0,4,2,1:T(8,128)S(1)}, u32[]{:S(2)}, u32[]{:S(2)}) collective-permute-start(f32[1,5,2,32,16,16]{3,5,0,4,2,1:T(8,128)} %get-tuple-element.148), channel_id=1, source_target_pairs={{0,7},{1,8},{2,9},{3,10},{4,11},{5,12},{6,13},{7,14},{8,15},{9,0},... | collective-permute-start | bytes 983048 | tf_op jit(solution)/shard_map/ppermute | solution.py:27
  594.6 94.9 %copy-start.5 = (f32[1,5,2,32,16,16]{3,5,0,4,2,1:T(8,128)S(1)}, f32[1,5,2,32,16,16]{3,5,0,4,2,1:T(8,128)}, u32[]{:S(2)}) copy-start(f32[1,5,2,32,16,16]{3,5,0,4,2,1:T(8,128)} %get-tuple-element.144) | copy-start | bytes 983044
  594.6 273.1 %collective-permute-start.9 = (f32[1,5,2,32,16,16]{3,5,0,4,2,1:T(8,128)S(1)}, f32[1,5,2,32,16,16]{3,5,0,4,2,1:T(8,128)S(1)}, u32[]{:S(2)}, u32[]{:S(2)}) collective-permute-start(f32[1,5,2,32,16,16]{3,5,0,4,2,1:T(8,128)S(1)} %copy-done.8), channel_id=1, source_target_pairs={{0,8},{1,9},{2,10},{3,11},{4,12},{5,13},{6,14},{7,15},{8,0},{9,1},... | collective-permute-start | bytes 983048 | tf_op jit(solution)/shard_map/ppermute | solution.py:27
  599.4 187.0 %copy-start.4 = (f32[1,5,2,32,16,16]{3,5,0,4,2,1:T(8,128)S(1)}, f32[1,5,2,32,16,16]{3,5,0,4,2,1:T(8,128)}, u32[]{:S(2)}) copy-start(f32[1,5,2,32,16,16]{3,5,0,4,2,1:T(8,128)} %get-tuple-element.143) | copy-start | bytes 983044
  599.4 332.4 %collective-permute-start.10 = (f32[1,5,2,32,16,16]{3,5,0,4,2,1:T(8,128)S(1)}, f32[1,5,2,32,16,16]{3,5,0,4,2,1:T(8,128)S(1)}, u32[]{:S(2)}, u32[]{:S(2)}) collective-permute-start(f32[1,5,2,32,16,16]{3,5,0,4,2,1:T(8,128)S(1)} %copy-done.7), channel_id=1, source_target_pairs={{0,9},{1,10},{2,11},{3,12},{4,13},{5,14},{6,15},{7,0},{8,1},{9,2},... | collective-permute-start | bytes 983048 | tf_op jit(solution)/shard_map/ppermute | solution.py:27
  626.7 241.1 %copy-start.3 = (f32[1,5,2,32,16,16]{3,5,0,4,2,1:T(8,128)S(1)}, f32[1,5,2,32,16,16]{3,5,0,4,2,1:T(8,128)}, u32[]{:S(2)}) copy-start(f32[1,5,2,32,16,16]{3,5,0,4,2,1:T(8,128)} %get-tuple-element.142) | copy-start | bytes 983044
  626.7 306.3 %collective-permute-start.11 = (f32[1,5,2,32,16,16]{3,5,0,4,2,1:T(8,128)S(1)}, f32[1,5,2,32,16,16]{3,5,0,4,2,1:T(8,128)S(1)}, u32[]{:S(2)}, u32[]{:S(2)}) collective-permute-start(f32[1,5,2,32,16,16]{3,5,0,4,2,1:T(8,128)S(1)} %copy-done.6), channel_id=1, source_target_pairs={{0,10},{1,11},{2,12},{3,13},{4,14},{5,15},{6,0},{7,1},{8,2},{9,3},... | collective-permute-start | bytes 983048 | tf_op jit(solution)/shard_map/ppermute | solution.py:27
  689.5 285.8 %collective-permute-start.12 = (f32[1,5,2,32,16,16]{3,5,0,4,2,1:T(8,128)S(1)}, f32[1,5,2,32,16,16]{3,5,0,4,2,1:T(8,128)S(1)}, u32[]{:S(2)}, u32[]{:S(2)}) collective-permute-start(f32[1,5,2,32,16,16]{3,5,0,4,2,1:T(8,128)S(1)} %copy-done.5), channel_id=1, source_target_pairs={{0,11},{1,12},{2,13},{3,14},{4,15},{5,0},{6,1},{7,2},{8,3},{9,4},{... | collective-permute-start | bytes 983048 | tf_op jit(solution)/shard_map/ppermute | solution.py:27
  786.4 190.1 %collective-permute-start.13 = (f32[1,5,2,32,16,16]{3,5,0,4,2,1:T(8,128)S(1)}, f32[1,5,2,32,16,16]{3,5,0,4,2,1:T(8,128)S(1)}, u32[]{:S(2)}, u32[]{:S(2)}) collective-permute-start(f32[1,5,2,32,16,16]{3,5,0,4,2,1:T(8,128)S(1)} %copy-done.4), channel_id=1, source_target_pairs={{0,12},{1,13},{2,14},{3,15},{4,0},{5,1},{6,2},{7,3},{8,4},{9,5},{1... | collective-permute-start | bytes 983048 | tf_op jit(solution)/shard_map/ppermute | solution.py:27
  867.7 110.0 %collective-permute-start.14 = (f32[1,5,2,32,16,16]{3,5,0,4,2,1:T(8,128)S(1)}, f32[1,5,2,32,16,16]{3,5,0,4,2,1:T(8,128)S(1)}, u32[]{:S(2)}, u32[]{:S(2)}) collective-permute-start(f32[1,5,2,32,16,16]{3,5,0,4,2,1:T(8,128)S(1)} %copy-done.3), channel_id=1, source_target_pairs={{0,13},{1,14},{2,15},{3,0},{4,1},{5,2},{6,3},{7,4},{8,5},{9,6},{10... | collective-permute-start | bytes 983048 | tf_op jit(solution)/shard_map/ppermute | solution.py:27
  931.8 88.4 %collective-permute-start.15 = (f32[1,5,2,32,16,16]{3,5,0,4,2,1:T(8,128)S(1)}, f32[1,5,2,32,16,16]{3,5,0,4,2,1:T(8,128)S(1)}, u32[]{:S(2)}, u32[]{:S(2)}) collective-permute-start(f32[1,5,2,32,16,16]{3,5,0,4,2,1:T(8,128)S(1)} %get-tuple-element.141), channel_id=1, source_target_pairs={{0,14},{1,15},{2,0},{3,1},{4,2},{5,3},{6,4},{7,5},{8,6},{9,7},{10,... | collective-permute-start | bytes 983048 | tf_op jit(solution)/shard_map/ppermute | solution.py:27
  933.0 91.0 %collective-permute-start.16 = (f32[1,5,2,32,16,16]{3,5,0,4,2,1:T(8,128)S(1)}, f32[1,5,2,32,16,16]{3,5,0,4,2,1:T(8,128)S(1)}, u32[]{:S(2)}, u32[]{:S(2)}) collective-permute-start(f32[1,5,2,32,16,16]{3,5,0,4,2,1:T(8,128)S(1)} %get-tuple-element.140), channel_id=1, source_target_pairs={{0,15},{1,0},{2,1},{3,2},{4,3},{5,4},{6,5},{7,6},{8,7},{9,8},{10,9... | collective-permute-start | bytes 983048 | tf_op jit(solution)/shard_map/ppermute | solution.py:27
  1067.7 5.1 copy-start.2
